TPU v7x, 32 devices: a whole 2x2x4 slice. The times are simulated.
32 devices in a mesh: gx: 4 (over z), gy: 4 (over y, x), gz: 2 (over core).
Axes of the slice: x: 2, y: 2, z: 4, core: 2. Of those that a mesh axis runs over, the one named last changes fastest.
Arguments:
- right_side: float32 [4, 96, 96, 48], P(None, 'gx', 'gy', 'gz'), may hold values from -6 to 6
- iterate: float32 [4, 96, 96, 48], P(None, 'gx', 'gy', 'gz'), may hold values from -6 to 6
- coefficient: float32 [96, 96, 48], P('gx', 'gy', 'gz'), may hold values from 0.1 to 2
- ordering: int32 [4, 4, 2, 216], P('gx', 'gy', 'gz'), may hold values from 0 to 215, as said below
- leaf_inverse: float32 [4, 4, 2, 125, 125], P('gx', 'gy', 'gz'), may hold values from -2 to 3
- leaf_first: float32 [4, 4, 2, 125, 50], P('gx', 'gy', 'gz'), may hold values from -0.5 to 0.5
- leaf_second: float32 [4, 4, 2, 125, 60], P('gx', 'gy', 'gz'), may hold values from -0.5 to 0.5
- leaf_top: float32 [4, 4, 2, 125, 72], P('gx', 'gy', 'gz'), may hold values from -0.5 to 0.5
- first_inverse: float32 [4, 4, 50, 50], P('gx', 'gy', 'gz'), may hold values from -2 to 3
- first_second: float32 [4, 4, 2, 25, 60], P('gx', 'gy', 'gz'), may hold values from -1.25 to 1.25
- first_top: float32 [4, 4, 2, 25, 72], P('gx', 'gy', 'gz'), may hold values from -1.25 to 1.25
- second_inverse: float32 [4, 240, 240], P('gx', ('gy', 'gz')), may hold values from -2 to 3
- second_top: float32 [4, 4, 2, 30, 72], P('gx', 'gy', 'gz'), may hold values from -1 to 1
- top_inverse: float32 [1152, 1152], P(('gx', 'gy', 'gz')), may hold values from -2 to 3
Outputs:
- correction: float32 [4, 96, 96, 48], P(None, 'gx', 'gy', 'gz')
Inputs may be any that keep to these rules, and one draw needn't show every extreme that they name: `ordering`: each device's row names each of its 216 coarse cells once (cell x 6^2 + y * 6 + z): first the 125 cells with x, y and z all below 5, then the 25 cells with z = 5 and x, y below it, then the 30 cells with y = 5 and x below it, then the 36 cells with x = 5, each group in any order.
All inputs are finite; a program needn't handle non-finite values.
Results may differ from a plain program's by a relative error of at most 0.0003.
Values sent between devices are 32-bit elements; how exact they have to be, the bound alone decides.
A program may use at most 64 MiB of HBM per device.

v0:
```python
import jax
import jax.numpy as jnp
from jax import lax
from jax.sharding import PartitionSpec as P

precise = lax.Precision.HIGHEST


def shifted(shard, axis, by):
    peers = lax.axis_size(axis)
    pairs = [(i, i + by) for i in range(peers) if 0 <= i + by < peers]
    return lax.ppermute(shard, axis, pairs)


def with_halo(cells, sides, width):
    for axis, dim in sides:
        count = lax.axis_size(axis)
        ends = count - 1
        head = lax.slice_in_dim(cells, 0, width, axis=dim)
        tail = lax.slice_in_dim(cells, cells.shape[dim] - width, cells.shape[dim], axis=dim)
        cells = jnp.concatenate(
            [
                lax.ppermute(tail, axis, [(i, (i + 1) % count) for i in range(ends)]),
                cells,
                lax.ppermute(head, axis, [((i + 1) % count, i) for i in range(ends)]),
            ],
            axis=dim,
        )
    return cells


def product(operand, matrix):
    return jnp.dot(operand, matrix, precision=precise, preferred_element_type=jnp.float32)


def product_back(operand, matrix):
    return lax.dot_general(
        operand,
        matrix,
        (((1,), (1,)), ((), ())),
        precision=precise,
        preferred_element_type=jnp.float32,
    )


def weigh(extended, dimension):
    length = extended.shape[dimension] - 1
    previous = lax.slice_in_dim(extended, 0, length, 2, dimension)
    centre = lax.slice_in_dim(extended, 1, length + 1, 2, dimension)
    following = lax.slice_in_dim(extended, 2, length + 1, 2, dimension)
    return 0.25 * previous + 0.5 * centre + 0.25 * following


def spread(extended, dimension):
    length = extended.shape[dimension] - 1
    current = lax.slice_in_dim(extended, 0, length, 1, dimension)
    following = lax.slice_in_dim(extended, 1, length + 1, 1, dimension)
    paired = jnp.stack([current, 0.5 * (current + following)], axis=dimension + 1)
    new_shape = list(current.shape)
    new_shape[dimension] = 2 * length
    return paired.reshape(new_shape)


def lower_rims(values):
    boundary = shifted(values[:, -1:], "gx", 1)
    values = jnp.concatenate([boundary, values], axis=1)
    boundary = shifted(values[:, :, -1:], "gy", 1)
    values = jnp.concatenate([boundary, values], axis=2)
    boundary = shifted(values[:, :, :, -1:], "gz", 1)
    return jnp.concatenate([boundary, values], axis=3)


def upper_rims(values):
    boundary = shifted(values[:, :1], "gx", -1)
    values = jnp.concatenate([values, boundary], axis=1)
    boundary = shifted(values[:, :, :1], "gy", -1)
    values = jnp.concatenate([values, boundary], axis=2)
    boundary = shifted(values[:, :, :, :1], "gz", -1)
    return jnp.concatenate([values, boundary], axis=3)


def restrict(values):
    extended = lower_rims(values)
    for dimension in (1, 2, 3):
        extended = weigh(extended, dimension)
    return extended


def prolong(values):
    extended = upper_rims(values)
    for dimension in (1, 2, 3):
        extended = spread(extended, dimension)
    return extended


def residual_of(right_side, iterate, coefficient):
    padded = with_halo(iterate, (("gx", 1), ("gy", 2), ("gz", 3)), 1)
    beside = padded[:, 2:, 1:-1, 1:-1] + padded[:, :-2, 1:-1, 1:-1]
    beside = beside + padded[:, 1:-1, 2:, 1:-1] + padded[:, 1:-1, :-2, 1:-1]
    beside = beside + padded[:, 1:-1, 1:-1, 2:] + padded[:, 1:-1, 1:-1, :-2]
    return right_side - ((6.0 + coefficient) * iterate - beside)


def per_device(
    right_side,
    iterate,
    coefficient,
    ordering,
    leaf_inverse,
    leaf_first,
    leaf_second,
    leaf_top,
    first_inverse,
    first_second,
    first_top,
    second_inverse,
    second_top,
    top_inverse,
):
    rhs_count = right_side.shape[0]
    leaf_size = leaf_inverse.shape[-1]
    first_size = first_second.shape[3]
    second_size = second_top.shape[3]
    top_size = top_inverse.shape[0]
    first_rows = first_inverse[0, 0]
    second_rows = second_inverse[0]
    first_start = lax.axis_index("gz") * first_size
    first_full = lax.all_gather(first_rows, "gz", axis=0, tiled=True)
    first_columns = lax.dynamic_slice_in_dim(first_full, first_start, first_size, 1)
    coarse = restrict(restrict(residual_of(right_side, iterate, coefficient)))
    coarse_side = coarse.shape[1]
    flattened = coarse.reshape(rhs_count, coarse_side**3)
    order_row = ordering.reshape(-1)
    chosen = jnp.take(flattened, order_row, axis=1)
    first_end = leaf_size + first_size
    second_end = first_end + second_size
    leaf_rhs = chosen[:, :leaf_size]
    first_rhs = chosen[:, leaf_size:first_end]
    second_rhs = chosen[:, first_end:second_end]
    top_rhs = chosen[:, second_end:]
    leaf_block = leaf_inverse[0, 0, 0]
    to_first = leaf_first[0, 0, 0]
    to_second = leaf_second[0, 0, 0]
    to_top = leaf_top[0, 0, 0]
    first_to_second = first_second[0, 0, 0]
    first_to_top = first_top[0, 0, 0]
    second_to_top = second_top[0, 0, 0]
    leaf_solved = product(leaf_rhs, leaf_block)
    toward = product(leaf_solved, to_first)
    arrived = shifted(toward[:, first_size:], "gz", -1)
    first_target = first_rhs - toward[:, :first_size] - arrived
    target_whole = lax.all_gather(first_target, "gz", axis=1, tiled=True)
    first_own = product(target_whole, first_columns)
    toward = product(leaf_solved, to_second) + product(first_own, first_to_second)
    arrived = shifted(toward[:, second_size:], "gy", -1)
    second_target = second_rhs - toward[:, :second_size] - arrived
    second_own = lax.psum_scatter(
        product(second_target, second_rows), ("gy", "gz"), scatter_dimension=1, tiled=True
    )
    toward = (
        product(leaf_solved, to_top)
        + product(first_own, first_to_top)
        + product(second_own, second_to_top)
    )
    arrived = shifted(toward[:, top_size:], "gx", -1)
    top_target = top_rhs - toward[:, :top_size] - arrived
    top_own = lax.psum_scatter(
        product(top_target, top_inverse), ("gx", "gy", "gz"), scatter_dimension=1, tiled=True
    )
    top_whole = lax.all_gather(top_own, ("gx", "gy", "gz"), axis=1, tiled=True)
    top_back = product_back(top_whole, top_inverse)
    top_lower = shifted(top_back, "gx", 1)
    top_pair = jnp.concatenate([top_back, top_lower], axis=1)
    second_gap = second_own - product_back(top_pair, second_to_top)
    second_whole = lax.all_gather(second_gap, ("gy", "gz"), axis=1, tiled=True)
    second_back = product_back(second_whole, second_rows)
    second_lower = shifted(second_back, "gy", 1)
    second_pair = jnp.concatenate([second_back, second_lower], axis=1)
    first_gap = (
        first_own
        - product_back(second_pair, first_to_second)
        - product_back(top_pair, first_to_top)
    )
    first_whole = lax.all_gather(first_gap, "gz", axis=1, tiled=True)
    first_back = product_back(first_whole, first_rows)
    first_lower = shifted(first_back, "gz", 1)
    first_pair = jnp.concatenate([first_back, first_lower], axis=1)
    leaf_gap = (
        leaf_solved - product_back(first_pair, to_first) - product_back(second_pair, to_second)
    )
    leaf_gap = leaf_gap - product_back(top_pair, to_top)
    leaf_back = product_back(leaf_gap, leaf_block)
    ordered = jnp.concatenate([leaf_back, first_back, second_back, top_back], axis=1)
    coarse_cells = jnp.zeros_like(ordered).at[:, order_row].set(ordered)
    coarse_grid = coarse_cells.reshape(rhs_count, coarse_side, coarse_side, coarse_side)
    return prolong(prolong(coarse_grid))


def solution(mesh):
    return jax.shard_map(
        per_device,
        mesh=mesh,
        in_specs=(
            P(None, "gx", "gy", "gz"),
            P(None, "gx", "gy", "gz"),
            P("gx", "gy", "gz"),
            P("gx", "gy", "gz", None),
            P("gx", "gy", "gz", None, None),
            P("gx", "gy", "gz", None, None),
            P("gx", "gy", "gz", None, None),
            P("gx", "gy", "gz", None, None),
            P("gx", "gy", "gz", None),
            P("gx", "gy", "gz", None, None),
            P("gx", "gy", "gz", None, None),
            P("gx", ("gy", "gz"), None),
            P("gx", "gy", "gz", None, None),
            P(("gx", "gy", "gz"), None),
        ),
        out_specs=P(None, "gx", "gy", "gz"),
        check_vma=False,
    )
```

profile of v0, /device:TPU:11, one launch (start us, length us, event | category | flops | bytes accessed | tf_op | source)
XLA Modules:
  0.0 293.7 jit_solution(13946960478446539935)
XLA Ops:
  0.9 2.1 collective-permute-start
  2.9 3.2 %collective-permute-start.1 = (f32[4,1,24,24]{3,2,1,0:T(8,128)S(1)}, f32[4,1,24,24]{3,2,1,0:T(8,128)S(1)}, u32[]{:S(2)}, u32[]{:S(2)}) collective-permute-start(f32[4,1,24,24]{3,2,1,0:T(8,128)S(1)} %get-tuple-element.9), channel_id=1, source_target_pairs={{0,8},{8,16},{16,24},{1,9},{9,17},{17,25},{2,10},{10,18},{18,26},{... | collective-permute-start | bytes 27656 | tf_op jit(solution)/shard_map/ppermute | solution.py:23
  6.2 1.6 copy.139
  8.5 1.7 copy.142
  11.2 2.2 collective-permute-start.2
  13.4 4.2 %collective-permute-start.3 = (f32[4,26,1,24]{1,3,2,0:T(8,128)S(1)}, f32[4,26,1,24]{1,3,2,0:T(8,128)S(1)}, u32[]{:S(2)}, u32[]{:S(2)}) collective-permute-start(f32[4,26,1,24]{1,3,2,0:T(8,128)S(1)} %get-tuple-element.7), channel_id=1, source_target_pairs={{0,2},{2,4},{4,6},{1,3},{3,5},{5,7},{8,10},{10,12},{12,14},{9,11},... | collective-permute-start | bytes 29960 | tf_op jit(solution)/shard_map/ppermute | solution.py:23
  19.3 4.4 %collective-permute-start.4 = (f32[4,26,26,1]{2,1,3,0:T(8,128)S(1)}, f32[4,26,26,1]{2,1,3,0:T(8,128)S(1)}, u32[]{:S(2)}, u32[]{:S(2)}) collective-permute-start(f32[4,26,26,1]{2,1,3,0:T(8,128)S(1)} %copy.147), channel_id=1, source_target_pairs={{1,0},{3,2},{5,4},{7,6},{9,8},{11,10},{13,12},{15,14},{17,16},{19,... | collective-permute-start | bytes 32456 | tf_op jit(solution)/shard_map/ppermute | solution.py:25
  25.2 2.7 copy.151
  28.3 9.4 %fusion.2 = f32[4,24,24,24]{1,3,2,0:T(8,128)S(1)} fusion(f32[4,24,24,24]{1,3,2,0:T(8,128)} %copy.151, f32[4,26,26,1]{1,3,2,0:T(1,128)S(1)} %copy.150, f32[4,26,1,24]{1,3,2,0:T(8,128)S(1)} %collective-permute-done.2, f32[4,26,1,24]{1,3,2,0:T(8,128)S(1)} %collective-permute-done.3, f32[4,1,24,24]{1,3,2,0:T(8,128)} %copy-done.1, ...), kind=kLoop, calls=%fused_computation.7 | loop fusion | flops 1437696 | bytes 778880 | tf_op jit(solution)/shard_map/sub | solution.py:101
  38.6 3.2 %collective-permute-start.6 = (f32[4,1,24,24]{3,2,1,0:T(8,128)S(1)}, f32[4,1,24,24]{3,2,1,0:T(8,128)S(1)}, u32[]{:S(2)}, u32[]{:S(2)}) collective-permute-start(f32[4,1,24,24]{3,2,1,0:T(8,128)S(1)} %copy.152), channel_id=1, source_target_pairs={{0,8},{8,16},{16,24},{1,9},{9,17},{17,25},{2,10},{10,18},{18,26},{... | collective-permute-start | bytes 27656 | tf_op jit(solution)/shard_map/ppermute | solution.py:12
  41.8 1.6 collective-permute-done.6
  44.2 4.9 %collective-permute-start.7 = (f32[4,25,1,24]{1,3,2,0:T(8,128)S(1)}, f32[4,25,1,24]{1,3,2,0:T(8,128)S(1)}, u32[]{:S(2)}, u32[]{:S(2)}) collective-permute-start(f32[4,25,1,24]{1,3,2,0:T(8,128)S(1)} %pad_maximum_fusion.35), channel_id=1, source_target_pairs={{0,2},{2,4},{4,6},{1,3},{3,5},{5,7},{8,10},{10,12},{12,14},{9,11},... | collective-permute-start | bytes 28808 | tf_op jit(solution)/shard_map/ppermute | solution.py:12
  51.8 3.8 %collective-permute-done.8 = f32[4,25,25,1]{2,1,3,0:T(8,128)S(1)} collective-permute-done((f32[4,25,25,1]{2,1,3,0:T(8,128)S(1)}, f32[4,25,25,1]{2,1,3,0:T(8,128)S(1)}, u32[]{:S(2)}, u32[]{:S(2)}) %collective-permute-start.8) | collective-permute-done | bytes 10032 | tf_op jit(solution)/shard_map/ppermute | solution.py:12
  55.8 1.8 maximum_maximum_fusion
  57.6 8.4 %slice.213 = f32[4,12,25,25]{1,3,2,0:T(8,128)} slice(f32[4,25,25,25]{1,3,2,0:T(8,128)S(1)} %maximum_maximum_fusion), slice={[0:4:1], [0:24:2], [0:25:1], [0:25:1]} | slice | bytes 240000 | tf_op jit(solution)/shard_map/slice | solution.py:48
  66.0 8.5 %slice.214 = f32[4,12,25,25]{1,3,2,0:T(8,128)} slice(f32[4,25,25,25]{1,3,2,0:T(8,128)S(1)} %maximum_maximum_fusion), slice={[0:4:1], [1:25:2], [0:25:1], [0:25:1]} | slice | bytes 240000 | tf_op jit(solution)/shard_map/slice | solution.py:49
  74.5 8.5 %slice.215 = f32[4,12,25,25]{1,3,2,0:T(8,128)} slice(f32[4,25,25,25]{1,3,2,0:T(8,128)S(1)} %maximum_maximum_fusion), slice={[0:4:1], [2:25:2], [0:25:1], [0:25:1]} | slice | bytes 240000 | tf_op jit(solution)/shard_map/slice | solution.py:50
  83.1 3.0 %multiply_add_fusion = f32[4,12,25,25]{1,3,2,0:T(8,128)S(1)} fusion(f32[4,12,25,25]{1,3,2,0:T(8,128)} %slice.215, f32[4,12,25,25]{1,3,2,0:T(8,128)} %slice.214, f32[4,12,25,25]{1,3,2,0:T(8,128)} %slice.213), kind=kLoop, calls=%fused_computation.3 | loop fusion | flops 150000 | bytes 480000 | tf_op jit(solution)/shard_map/add | solution.py:51
  87.2 3.2 %collective-permute-start.9 = (f32[4,1,12,12]{1,3,2,0:T(8,128)S(1)}, f32[4,1,12,12]{1,3,2,0:T(8,128)S(1)}, u32[]{:S(2)}, u32[]{:S(2)}) collective-permute-start(f32[4,1,12,12]{1,3,2,0:T(8,128)S(1)} %slice.265), channel_id=1, source_target_pairs={{0,8},{8,16},{16,24},{1,9},{9,17},{17,25},{2,10},{10,18},{18,26},{... | collective-permute-start | bytes 6920 | tf_op jit(solution)/shard_map/ppermute | solution.py:12
  90.4 1.9 all-gather
  92.3 7.3 %collective-permute-done.9 = f32[4,1,12,12]{1,3,2,0:T(8,128)S(1)} collective-permute-done((f32[4,1,12,12]{1,3,2,0:T(8,128)S(1)}, f32[4,1,12,12]{1,3,2,0:T(8,128)S(1)}, u32[]{:S(2)}, u32[]{:S(2)}) %collective-permute-start.9) | collective-permute-done | bytes 2336 | tf_op jit(solution)/shard_map/ppermute | solution.py:12
  99.7 4.9 %collective-permute-start.10 = (f32[4,13,1,12]{1,3,2,0:T(8,128)S(1)}, f32[4,13,1,12]{1,3,2,0:T(8,128)S(1)}, u32[]{:S(2)}, u32[]{:S(2)}) collective-permute-start(f32[4,13,1,12]{1,3,2,0:T(8,128)S(1)} %pad_maximum_fusion.39), channel_id=1, source_target_pairs={{0,2},{2,4},{4,6},{1,3},{3,5},{5,7},{8,10},{10,12},{12,14},{9,11},... | collective-permute-start | bytes 7496 | tf_op jit(solution)/shard_map/ppermute | solution.py:12
  115.0 2.6 collective-permute-start.12
  118.5 1.8 all-gather.1
  120.8 1.9 collective-permute-start.13
  122.9 3.7 %collective-permute-done.13 = f32[4,30]{1,0:T(4,128)S(1)} collective-permute-done((f32[4,30]{1,0:T(4,128)S(1)}, f32[4,30]{1,0:T(4,128)S(1)}, u32[]{:S(2)}, u32[]{:S(2)}) %collective-permute-start.13) | collective-permute-done | bytes 512 | tf_op jit(solution)/shard_map/ppermute | solution.py:12
  126.8 11.4 %all-reduce = f32[4,240]{1,0:T(4,128)S(1)} all-reduce(f32[4,240]{1,0:T(4,128)S(1)} %fusion.36), channel_id=3, replica_groups=mesh['gx'=4,'gy'=4,'gz'=2] {'gy','gz'}, use_global_device_ids=true, to_apply=%region_0.1.clone | all-reduce | flops 960 | bytes 7680
  138.5 2.1 collective-permute-start.14
  140.6 2.2 collective-permute-done.14
  143.1 40.6 %all-reduce.1 = f32[4,1152]{1,0:T(4,128)S(1)} all-reduce(f32[4,1152]{1,0:T(4,128)S(1)} %fusion.68), channel_id=4, replica_groups=mesh['gx'=4,'gy'=4,'gz'=2] {'gx','gy','gz'}, use_global_device_ids=true, to_apply=%region_1.2.clone | all-reduce | flops 4608 | bytes 36864
  183.8 32.4 %all-gather.2 = f32[32,36,4]{1,2,0:T(4,128)S(1)} all-gather(f32[1,36,4]{1,2,0:T(4,128)S(1)} %dynamic-slice_bitcast_fusion), channel_id=1, replica_groups=mesh['gx'=4,'gy'=4,'gz'=2] {'gx','gy','gz'}, dimensions={0}, use_global_device_ids=true | all-gather | bytes 19008 | tf_op jit(solution)/shard_map/all_gather | solution.py:170
  216.5 2.0 collective-permute-start.15
  218.5 6.9 %collective-permute-done.15 = f32[4,36]{1,0:T(4,128)S(1)} collective-permute-done((f32[4,36]{1,0:T(4,128)S(1)}, f32[4,36]{1,0:T(4,128)S(1)}, u32[]{:S(2)}, u32[]{:S(2)}) %collective-permute-start.15) | collective-permute-done | bytes 608 | tf_op jit(solution)/shard_map/ppermute | solution.py:12
  225.6 13.6 %all-gather.3 = f32[8,30,4]{1,2,0:T(4,128)S(1)} all-gather(f32[1,30,4]{1,2,0:T(4,128)S(1)} %fusion.9), channel_id=1, replica_groups=mesh['gx'=4,'gy'=4,'gz'=2] {'gy','gz'}, dimensions={0}, use_global_device_ids=true | all-gather | bytes 4320 | tf_op jit(solution)/shard_map/all_gather | solution.py:175
  239.4 3.1 %collective-permute-start.16 = (f32[4,30]{1,0:T(4,128)S(1)}, f32[4,30]{1,0:T(4,128)S(1)}, u32[]{:S(2)}, u32[]{:S(2)}) collective-permute-start(f32[4,30]{1,0:T(4,128)S(1)} %fusion.34), channel_id=1, source_target_pairs={{0,2},{2,4},{4,6},{1,3},{3,5},{5,7},{8,10},{10,12},{12,14},{9,11},... | collective-permute-start | bytes 1448 | tf_op jit(solution)/shard_map/ppermute | solution.py:12
  244.1 2.8 all-gather.4
  248.7 1.6 collective-permute-done.17
  252.4 1.9 collective-permute-start.18
  254.3 2.5 collective-permute-done.18
  256.9 1.9 collective-permute-start.19
  258.8 3.4 %collective-permute-done.19 = f32[4,7,1,6]{3,2,1,0:T(1,128)S(1)} collective-permute-done((f32[4,7,1,6]{3,2,1,0:T(1,128)S(1)}, f32[4,7,1,6]{3,2,1,0:T(1,128)S(1)}, u32[]{:S(2)}, u32[]{:S(2)}) %collective-permute-start.19) | collective-permute-done | bytes 704 | tf_op jit(solution)/shard_map/ppermute | solution.py:12
  262.3 4.4 %collective-permute-start.20 = (f32[4,7,7,1]{3,2,1,0:T(8,128)S(1)}, f32[4,7,7,1]{3,2,1,0:T(8,128)S(1)}, u32[]{:S(2)}, u32[]{:S(2)}) collective-permute-start(f32[4,7,7,1]{3,2,1,0:T(8,128)S(1)} %pad_maximum_fusion.26), channel_id=1, source_target_pairs={{1,0},{3,2},{5,4},{7,6},{9,8},{11,10},{13,12},{15,14},{17,16},{19,... | collective-permute-start | bytes 2360 | tf_op jit(solution)/shard_map/ppermute | solution.py:12
  269.0 1.9 collective-permute-start.21
  270.9 2.6 collective-permute-done.21
  273.7 1.9 collective-permute-start.22
  275.6 8.4 %collective-permute-done.22 = f32[4,13,1,12]{2,0,3,1:T(4,128)S(1)} collective-permute-done((f32[4,13,1,12]{2,0,3,1:T(4,128)S(1)}, f32[4,13,1,12]{2,0,3,1:T(4,128)S(1)}, u32[]{:S(2)}, u32[]{:S(2)}) %collective-permute-start.22) | collective-permute-done | bytes 2528 | tf_op jit(solution)/shard_map/ppermute | solution.py:12
  284.1 4.3 %collective-permute-start.23 = (f32[4,13,13,1]{2,0,3,1:T(4,128)S(1)}, f32[4,13,13,1]{2,0,3,1:T(4,128)S(1)}, u32[]{:S(2)}, u32[]{:S(2)}) collective-permute-start(f32[4,13,13,1]{2,0,3,1:T(4,128)S(1)} %pad_maximum_fusion.40), channel_id=1, source_target_pairs={{1,0},{3,2},{5,4},{7,6},{9,8},{11,10},{13,12},{15,14},{17,16},{19,... | collective-permute-start | bytes 8120 | tf_op jit(solution)/shard_map/ppermute | solution.py:12
  292.3 1.4 copy.181
  (162 shorter events, 36.2 us)
Async XLA Ops:
  0.0 142.9 %copy-start = (f32[36,1152]{1,0:T(8,128)S(1)}, f32[36,1152]{1,0:T(8,128)}, u32[]{:S(2)}) copy-start(f32[36,1152]{1,0:T(8,128)} %param.27) | copy-start | bytes 497668
  0.9 6.9 %collective-permute-start = (f32[4,1,24,24]{3,2,1,0:T(8,128)S(1)}, f32[4,1,24,24]{3,2,1,0:T(8,128)S(1)}, u32[]{:S(2)}, u32[]{:S(2)}) collective-permute-start(f32[4,1,24,24]{3,2,1,0:T(8,128)S(1)} %get-tuple-element.10), channel_id=1, source_target_pairs={{8,0},{16,8},{24,16},{9,1},{17,9},{25,17},{10,2},{18,10},{26,18},{... | collective-permute-start | bytes 27656 | tf_op jit(solution)/shard_map/ppermute | solution.py:25
  2.9 5.5 %collective-permute-start.1 = (f32[4,1,24,24]{3,2,1,0:T(8,128)S(1)}, f32[4,1,24,24]{3,2,1,0:T(8,128)S(1)}, u32[]{:S(2)}, u32[]{:S(2)}) collective-permute-start(f32[4,1,24,24]{3,2,1,0:T(8,128)S(1)} %get-tuple-element.9), channel_id=1, source_target_pairs={{0,8},{8,16},{16,24},{1,9},{9,17},{17,25},{2,10},{10,18},{18,26},{... | collective-permute-start | bytes 27656 | tf_op jit(solution)/shard_map/ppermute | solution.py:23
  8.5 10.7 %copy-start.1 = (f32[4,1,24,24]{1,3,2,0:T(8,128)}, f32[4,1,24,24]{1,3,2,0:T(8,128)S(1)}, u32[]{:S(2)}) copy-start(f32[4,1,24,24]{1,3,2,0:T(8,128)S(1)} %copy.141) | copy-start | bytes 27652
  10.1 8.5 %copy-start.2 = (f32[4,1,24,24]{1,3,2,0:T(8,128)S(1)}, f32[4,1,24,24]{1,3,2,0:T(8,128)}, u32[]{:S(2)}) copy-start(f32[4,1,24,24]{1,3,2,0:T(8,128)} %copy.142) | copy-start | bytes 27652
  11.2 6.3 %collective-permute-start.2 = (f32[4,26,1,24]{1,3,2,0:T(8,128)S(1)}, f32[4,26,1,24]{1,3,2,0:T(8,128)S(1)}, u32[]{:S(2)}, u32[]{:S(2)}) collective-permute-start(f32[4,26,1,24]{1,3,2,0:T(8,128)S(1)} %get-tuple-element.8), channel_id=1, source_target_pairs={{2,0},{4,2},{6,4},{3,1},{5,3},{7,5},{10,8},{12,10},{14,12},{11,9},... | collective-permute-start | bytes 29960 | tf_op jit(solution)/shard_map/ppermute | solution.py:25
  13.4 11.8 %copy-start.4 = (f32[24,24,24]{2,1,0:T(8,128)S(1)}, f32[24,24,24]{2,1,0:T(8,128)}, u32[]{:S(2)}) copy-start(f32[24,24,24]{2,1,0:T(8,128)} %param.16) | copy-start | bytes 165892
  13.4 5.3 %collective-permute-start.3 = (f32[4,26,1,24]{1,3,2,0:T(8,128)S(1)}, f32[4,26,1,24]{1,3,2,0:T(8,128)S(1)}, u32[]{:S(2)}, u32[]{:S(2)}) collective-permute-start(f32[4,26,1,24]{1,3,2,0:T(8,128)S(1)} %get-tuple-element.7), channel_id=1, source_target_pairs={{0,2},{2,4},{4,6},{1,3},{3,5},{5,7},{8,10},{10,12},{12,14},{9,11},... | collective-permute-start | bytes 29960 | tf_op jit(solution)/shard_map/ppermute | solution.py:23
  19.3 8.7 %collective-permute-start.4 = (f32[4,26,26,1]{2,1,3,0:T(8,128)S(1)}, f32[4,26,26,1]{2,1,3,0:T(8,128)S(1)}, u32[]{:S(2)}, u32[]{:S(2)}) collective-permute-start(f32[4,26,26,1]{2,1,3,0:T(8,128)S(1)} %copy.147), channel_id=1, source_target_pairs={{1,0},{3,2},{5,4},{7,6},{9,8},{11,10},{13,12},{15,14},{17,16},{19,... | collective-permute-start | bytes 32456 | tf_op jit(solution)/shard_map/ppermute | solution.py:25
  23.9 4.3 %collective-permute-start.5 = (f32[4,26,26,1]{2,1,3,0:T(8,128)S(1)}, f32[4,26,26,1]{2,1,3,0:T(8,128)S(1)}, u32[]{:S(2)}, u32[]{:S(2)}) collective-permute-start(f32[4,26,26,1]{2,1,3,0:T(8,128)S(1)} %copy.149), channel_id=1, source_target_pairs={{0,1},{2,3},{4,5},{6,7},{8,9},{10,11},{12,13},{14,15},{16,17},{18,... | collective-permute-start | bytes 32456 | tf_op jit(solution)/shard_map/ppermute | solution.py:23
  38.6 4.8 %collective-permute-start.6 = (f32[4,1,24,24]{3,2,1,0:T(8,128)S(1)}, f32[4,1,24,24]{3,2,1,0:T(8,128)S(1)}, u32[]{:S(2)}, u32[]{:S(2)}) collective-permute-start(f32[4,1,24,24]{3,2,1,0:T(8,128)S(1)} %copy.152), channel_id=1, source_target_pairs={{0,8},{8,16},{16,24},{1,9},{9,17},{17,25},{2,10},{10,18},{18,26},{... | collective-permute-start | bytes 27656 | tf_op jit(solution)/shard_map/ppermute | solution.py:12
  44.1 11.6 %copy-start.3 = (f32[4,1,24,24]{1,3,2,0:T(8,128)}, f32[4,1,24,24]{1,3,2,0:T(8,128)S(1)}, u32[]{:S(2)}) copy-start(f32[4,1,24,24]{1,3,2,0:T(8,128)S(1)} %copy.153) | copy-start | bytes 27652
  44.1 5.0 %copy-start.14 = (s32[1,1,1,216]{3,2,1,0:T(1,128)S(1)}, s32[1,1,1,216]{3,2,1,0:T(1,128)}, u32[]{:S(2)}) copy-start(s32[1,1,1,216]{3,2,1,0:T(1,128)} %param.17) | copy-start | bytes 2596
  44.2 6.0 %collective-permute-start.7 = (f32[4,25,1,24]{1,3,2,0:T(8,128)S(1)}, f32[4,25,1,24]{1,3,2,0:T(8,128)S(1)}, u32[]{:S(2)}, u32[]{:S(2)}) collective-permute-start(f32[4,25,1,24]{1,3,2,0:T(8,128)S(1)} %pad_maximum_fusion.35), channel_id=1, source_target_pairs={{0,2},{2,4},{4,6},{1,3},{3,5},{5,7},{8,10},{10,12},{12,14},{9,11},... | collective-permute-start | bytes 28808 | tf_op jit(solution)/shard_map/ppermute | solution.py:12
  50.5 5.1 %collective-permute-start.8 = (f32[4,25,25,1]{2,1,3,0:T(8,128)S(1)}, f32[4,25,25,1]{2,1,3,0:T(8,128)S(1)}, u32[]{:S(2)}, u32[]{:S(2)}) collective-permute-start(f32[4,25,25,1]{2,1,3,0:T(8,128)S(1)} %copy.154), channel_id=1, source_target_pairs={{0,1},{2,3},{4,5},{6,7},{8,9},{10,11},{12,13},{14,15},{16,17},{18,... | collective-permute-start | bytes 30008 | tf_op jit(solution)/shard_map/ppermute | solution.py:12
  86.9 3.5 %copy-start.13 = (f32[1,1,25,50]{3,1,2,0:T(1,128)S(1)}, f32[1,1,25,50]{3,1,2,0:T(1,128)}, u32[]{:S(2)}) copy-start(f32[1,1,25,50]{3,1,2,0:T(1,128)} %param.22) | copy-start | bytes 15004
  87.0 20.1 %copy-start.15 = (u32[32]{0:T(128)S(1)}, u32[32]{0:T(128)}, u32[]{:S(2)}) copy-start(u32[32]{0:T(128)} %constant.32) | copy-start | bytes 388
  87.2 12.4 %collective-permute-start.9 = (f32[4,1,12,12]{1,3,2,0:T(8,128)S(1)}, f32[4,1,12,12]{1,3,2,0:T(8,128)S(1)}, u32[]{:S(2)}, u32[]{:S(2)}) collective-permute-start(f32[4,1,12,12]{1,3,2,0:T(8,128)S(1)} %slice.265), channel_id=1, source_target_pairs={{0,8},{8,16},{16,24},{1,9},{9,17},{17,25},{2,10},{10,18},{18,26},{... | collective-permute-start | bytes 6920 | tf_op jit(solution)/shard_map/ppermute | solution.py:12
  99.7 5.9 %collective-permute-start.10 = (f32[4,13,1,12]{1,3,2,0:T(8,128)S(1)}, f32[4,13,1,12]{1,3,2,0:T(8,128)S(1)}, u32[]{:S(2)}, u32[]{:S(2)}) collective-permute-start(f32[4,13,1,12]{1,3,2,0:T(8,128)S(1)} %pad_maximum_fusion.39), channel_id=1, source_target_pairs={{0,2},{2,4},{4,6},{1,3},{3,5},{5,7},{8,10},{10,12},{12,14},{9,11},... | collective-permute-start | bytes 7496 | tf_op jit(solution)/shard_map/ppermute | solution.py:12
  105.7 3.8 %collective-permute-start.11 = (f32[4,13,13,1]{1,3,2,0:T(1,128)S(1)}, f32[4,13,13,1]{1,3,2,0:T(1,128)S(1)}, u32[]{:S(2)}, u32[]{:S(2)}) collective-permute-start(f32[4,13,13,1]{1,3,2,0:T(1,128)S(1)} %pad_maximum_fusion.42), channel_id=1, source_target_pairs={{0,1},{2,3},{4,5},{6,7},{8,9},{10,11},{12,13},{14,15},{16,17},{18,... | collective-permute-start | bytes 8120 | tf_op jit(solution)/shard_map/ppermute | solution.py:12
  112.7 2.0 copy-start.5
  112.7 2.1 copy-start.9
  112.7 5.0 %copy-start.6 = (f32[1,1,1,125,72]{3,4,2,1,0:T(8,128)S(1)}, f32[1,1,1,125,72]{3,4,2,1,0:T(8,128)}, u32[]{:S(2)}) copy-start(f32[1,1,1,125,72]{3,4,2,1,0:T(8,128)} %param.21) | copy-start | bytes 108004
  112.7 5.1 %copy-start.8 = (f32[1,1,1,125,60]{3,2,4,1,0:T(1,128)S(1)}, f32[1,1,1,125,60]{3,2,4,1,0:T(1,128)}, u32[]{:S(2)}) copy-start(f32[1,1,1,125,60]{3,2,4,1,0:T(1,128)} %param.20) | copy-start | bytes 90004
  112.7 7.9 %copy-start.10 = (f32[1,1,1,25,60]{4,2,3,1,0:T(1,128)S(1)}, f32[1,1,1,25,60]{4,2,3,1,0:T(1,128)}, u32[]{:S(2)}) copy-start(f32[1,1,1,25,60]{4,2,3,1,0:T(1,128)} %param.23) | copy-start | bytes 18004
  112.7 10.0 %copy-start.11 = (f32[1,1,1,25,72]{4,2,3,1,0:T(1,128)S(1)}, f32[1,1,1,25,72]{4,2,3,1,0:T(1,128)}, u32[]{:S(2)}) copy-start(f32[1,1,1,25,72]{4,2,3,1,0:T(1,128)} %param.24) | copy-start | bytes 21604
  112.7 13.9 %copy-start.7 = (f32[1,30,240]{2,0,1:T(1,128)S(1)}, f32[1,30,240]{2,0,1:T(1,128)}, u32[]{:S(2)}) copy-start(f32[1,30,240]{2,0,1:T(1,128)} %param.25) | copy-start | bytes 86404
  112.7 25.5 %copy-start.12 = (f32[1,1,1,30,72]{4,2,3,1,0:T(1,128)S(1)}, f32[1,1,1,30,72]{4,2,3,1,0:T(1,128)}, u32[]{:S(2)}) copy-start(f32[1,1,1,30,72]{4,2,3,1,0:T(1,128)} %param.26) | copy-start | bytes 25924
  115.0 3.4 %collective-permute-start.12 = (f32[4,25]{1,0:T(4,128)S(1)}, f32[4,25]{1,0:T(4,128)S(1)}, u32[]{:S(2)}, u32[]{:S(2)}) collective-permute-start(f32[4,25]{1,0:T(4,128)S(1)} %slice.237), channel_id=1, source_target_pairs={{1,0},{3,2},{5,4},{7,6},{9,8},{11,10},{13,12},{15,14},{17,16},{19,... | collective-permute-start | bytes 1208 | tf_op jit(solution)/shard_map/ppermute | solution.py:12
  120.8 5.8 %collective-permute-start.13 = (f32[4,30]{1,0:T(4,128)S(1)}, f32[4,30]{1,0:T(4,128)S(1)}, u32[]{:S(2)}, u32[]{:S(2)}) collective-permute-start(f32[4,30]{1,0:T(4,128)S(1)} %slice.240), channel_id=1, source_target_pairs={{2,0},{4,2},{6,4},{3,1},{5,3},{7,5},{10,8},{12,10},{14,12},{11,9},... | collective-permute-start | bytes 1448 | tf_op jit(solution)/shard_map/ppermute | solution.py:12
  138.5 4.3 %collective-permute-start.14 = (f32[4,36]{1,0:T(4,128)S(1)}, f32[4,36]{1,0:T(4,128)S(1)}, u32[]{:S(2)}, u32[]{:S(2)}) collective-permute-start(f32[4,36]{1,0:T(4,128)S(1)} %slice.243), channel_id=1, source_target_pairs={{8,0},{16,8},{24,16},{9,1},{17,9},{25,17},{10,2},{18,10},{26,18},{... | collective-permute-start | bytes 1736 | tf_op jit(solution)/shard_map/ppermute | solution.py:12
  216.5 8.9 %collective-permute-start.15 = (f32[4,36]{1,0:T(4,128)S(1)}, f32[4,36]{1,0:T(4,128)S(1)}, u32[]{:S(2)}, u32[]{:S(2)}) collective-permute-start(f32[4,36]{1,0:T(4,128)S(1)} %fusion.86), channel_id=1, source_target_pairs={{0,8},{8,16},{16,24},{1,9},{9,17},{17,25},{2,10},{10,18},{18,26},{... | collective-permute-start | bytes 1736 | tf_op jit(solution)/shard_map/ppermute | solution.py:12
  239.4 4.3 %collective-permute-start.16 = (f32[4,30]{1,0:T(4,128)S(1)}, f32[4,30]{1,0:T(4,128)S(1)}, u32[]{:S(2)}, u32[]{:S(2)}) collective-permute-start(f32[4,30]{1,0:T(4,128)S(1)} %fusion.34), channel_id=1, source_target_pairs={{0,2},{2,4},{4,6},{1,3},{3,5},{5,7},{8,10},{10,12},{12,14},{9,11},... | collective-permute-start | bytes 1448 | tf_op jit(solution)/shard_map/ppermute | solution.py:12
  247.2 3.1 %collective-permute-start.17 = (f32[4,25]{1,0:T(4,128)S(1)}, f32[4,25]{1,0:T(4,128)S(1)}, u32[]{:S(2)}, u32[]{:S(2)}) collective-permute-start(f32[4,25]{1,0:T(4,128)S(1)} %fusion.50), channel_id=1, source_target_pairs={{0,1},{2,3},{4,5},{6,7},{8,9},{10,11},{12,13},{14,15},{16,17},{18,... | collective-permute-start | bytes 1208 | tf_op jit(solution)/shard_map/ppermute | solution.py:12
  252.4 4.5 %collective-permute-start.18 = (f32[4,1,6,6]{3,2,1,0:T(8,128)S(1)}, f32[4,1,6,6]{3,2,1,0:T(8,128)S(1)}, u32[]{:S(2)}, u32[]{:S(2)}) collective-permute-start(f32[4,1,6,6]{3,2,1,0:T(8,128)S(1)} %slice.270), channel_id=1, source_target_pairs={{8,0},{16,8},{24,16},{9,1},{17,9},{25,17},{10,2},{18,10},{26,18},{... | collective-permute-start | bytes 1736 | tf_op jit(solution)/shard_map/ppermute | solution.py:12
  256.9 5.4 %collective-permute-start.19 = (f32[4,7,1,6]{3,2,1,0:T(1,128)S(1)}, f32[4,7,1,6]{3,2,1,0:T(1,128)S(1)}, u32[]{:S(2)}, u32[]{:S(2)}) collective-permute-start(f32[4,7,1,6]{3,2,1,0:T(1,128)S(1)} %slice.271), channel_id=1, source_target_pairs={{2,0},{4,2},{6,4},{3,1},{5,3},{7,5},{10,8},{12,10},{14,12},{11,9},... | collective-permute-start | bytes 2024 | tf_op jit(solution)/shard_map/ppermute | solution.py:12
  262.3 5.3 %collective-permute-start.20 = (f32[4,7,7,1]{3,2,1,0:T(8,128)S(1)}, f32[4,7,7,1]{3,2,1,0:T(8,128)S(1)}, u32[]{:S(2)}, u32[]{:S(2)}) collective-permute-start(f32[4,7,7,1]{3,2,1,0:T(8,128)S(1)} %pad_maximum_fusion.26), channel_id=1, source_target_pairs={{1,0},{3,2},{5,4},{7,6},{9,8},{11,10},{13,12},{15,14},{17,16},{19,... | collective-permute-start | bytes 2360 | tf_op jit(solution)/shard_map/ppermute | solution.py:12
  269.0 4.6 %collective-permute-start.21 = (f32[4,1,12,12]{2,0,3,1:T(4,128)S(1)}, f32[4,1,12,12]{2,0,3,1:T(4,128)S(1)}, u32[]{:S(2)}, u32[]{:S(2)}) collective-permute-start(f32[4,1,12,12]{2,0,3,1:T(4,128)S(1)} %slice.278), channel_id=1, source_target_pairs={{8,0},{16,8},{24,16},{9,1},{17,9},{25,17},{10,2},{18,10},{26,18},{... | collective-permute-start | bytes 6920 | tf_op jit(solution)/shard_map/ppermute | solution.py:12
  273.7 10.4 %collective-permute-start.22 = (f32[4,13,1,12]{2,0,3,1:T(4,128)S(1)}, f32[4,13,1,12]{2,0,3,1:T(4,128)S(1)}, u32[]{:S(2)}, u32[]{:S(2)}) collective-permute-start(f32[4,13,1,12]{2,0,3,1:T(4,128)S(1)} %pad_maximum_fusion.22), channel_id=1, source_target_pairs={{2,0},{4,2},{6,4},{3,1},{5,3},{7,5},{10,8},{12,10},{14,12},{11,9},... | collective-permute-start | bytes 7496 | tf_op jit(solution)/shard_map/ppermute | solution.py:12
  284.1 5.1 %collective-permute-start.23 = (f32[4,13,13,1]{2,0,3,1:T(4,128)S(1)}, f32[4,13,13,1]{2,0,3,1:T(4,128)S(1)}, u32[]{:S(2)}, u32[]{:S(2)}) collective-permute-start(f32[4,13,13,1]{2,0,3,1:T(4,128)S(1)} %pad_maximum_fusion.40), channel_id=1, source_target_pairs={{1,0},{3,2},{5,4},{7,6},{9,8},{11,10},{13,12},{15,14},{17,16},{19,... | collective-permute-start | bytes 8120 | tf_op jit(solution)/shard_map/ppermute | solution.py:12
where the time goes:
time: 295 us; the launch traced here: 294 us
  blocking collectives  105 us (36%)
  starting transfers between devices  65.4 us (22%)
  waiting for transfers between devices  52 us (18%)
  local copies, waits for them, and re-layouts  48.2 us (16%)
  other arithmetic  18.5 us (6%)
  matrix products  3.58 us (1%)
    unnamed x2, blocking collectives  52.1 us
    ppermute x18, waiting for transfers between devices, shifted(): return lax.ppermute(shard, axis, pairs)  50.9 us
    ppermute x18, starting transfers between devices, shifted(): return lax.ppermute(shard, axis, pairs)  48 us
    all_gather x1, blocking collectives, per_device(): top_whole = lax.all_gather(top_own, ('gx', 'gy', 'gz'), axis=1, tiled=True)  32.4 us
    all_gather x1, blocking collectives, per_device(): second_whole = lax.all_gather(second_gap, ('gy', 'gz'), axis=1, tiled=True)  13.6 us
    slice x4, local copies, waits for them, and re-layouts, weigh(): following = lax.slice_in_dim(extended, 2, length + 1, 2, dimension)  9.86 us
    slice x4, local copies, waits for them, and re-layouts, weigh(): centre = lax.slice_in_dim(extended, 1, length + 1, 2, dimension)  9.85 us
    slice x4, local copies, waits for them, and re-layouts, weigh(): previous = lax.slice_in_dim(extended, 0, length, 2, dimension)  9.6 us
  transfers between devices with their start and end apart: 24, of which 19 were waited for; matrix products, arithmetic and copies ran while one was open for 2% of the time, Pallas kernels for 0%

commit v1 on v0

--- a/solution.py
+++ b/solution.py
@@ -167,7 +167,10 @@
     top_own = lax.psum_scatter(
         product(top_target, top_inverse), ("gx", "gy", "gz"), scatter_dimension=1, tiled=True
     )
-    top_whole = lax.all_gather(top_own, ("gx", "gy", "gz"), axis=1, tiled=True)
+    size = lax.axis_size(("gx", "gy", "gz"))
+    parts = jnp.stack([top_own for _ in range(size)])
+    parts = lax.all_to_all(parts, ("gx", "gy", "gz"), split_axis=0, concat_axis=0)
+    top_whole = jnp.concatenate(parts, axis=1)
     top_back = product_back(top_whole, top_inverse)
     top_lower = shifted(top_back, "gx", 1)
     top_pair = jnp.concatenate([top_back, top_lower], axis=1)

time: 295 us -> 268 us (0.908)
  blocking collectives: 105 us -> 81.2 us
  waiting for transfers between devices: 52 us -> 47.2 us
    all_gather x1 -> x0, blocking collectives: 32.4 us -> none  [per_device(): top_whole = lax.all_gather(top_own, ('gx', 'gy', 'gz'), axis=1, tiled=True)]
    all_to_all x0 -> x1, blocking collectives: none -> 12.3 us  [per_device(): lax.all_to_all(parts, ('gx', 'gy', 'gz'), split_axis=0, concat_axis=0)]
    ppermute x18, waiting for transfers between devices: 50.9 us -> 46.1 us  [shifted(): return lax.ppermute(shard, axis, pairs)]
    all_gather x1, blocking collectives: 13.6 us -> 10.3 us  [per_device(): second_whole = lax.all_gather(second_gap, ('gy', 'gz'), axis=1, tiled=True)]
  transfers between devices with their start and end apart: 24 -> 24, of which waited for: 19 -> 19; matrix products, arithmetic and copies ran while one was open for 2% -> 3% of each run, Pallas kernels for 0% -> 0%
where the time goes in v1:
time: 268 us; the launch traced here: 267 us
  blocking collectives  81.2 us (30%)
  starting transfers between devices  65.7 us (25%)
  local copies, waits for them, and re-layouts  49 us (18%)
  waiting for transfers between devices  47.2 us (18%)
  other arithmetic  19.2 us (7%)
  matrix products  3.58 us (1%)
    unnamed x2, blocking collectives  52.1 us
    ppermute x18, starting transfers between devices, shifted(): return lax.ppermute(shard, axis, pairs)  48.4 us
    ppermute x18, waiting for transfers between devices, shifted(): return lax.ppermute(shard, axis, pairs)  46.1 us
    all_to_all x1, blocking collectives, per_device(): lax.all_to_all(parts, ('gx', 'gy', 'gz'), split_axis=0, concat_axis=0)  12.3 us
    all_gather x1, blocking collectives, per_device(): second_whole = lax.all_gather(second_gap, ('gy', 'gz'), axis=1, tiled=True)  10.3 us
    slice x4, local copies, waits for them, and re-layouts, weigh(): following = lax.slice_in_dim(extended, 2, length + 1, 2, dimension)  9.85 us
    slice x4, local copies, waits for them, and re-layouts, weigh(): centre = lax.slice_in_dim(extended, 1, length + 1, 2, dimension)  9.85 us
    slice x4, local copies, waits for them, and re-layouts, weigh(): previous = lax.slice_in_dim(extended, 0, length, 2, dimension)  9.58 us
  transfers between devices with their start and end apart: 24, of which 19 were waited for; matrix products, arithmetic and copies ran while one was open for 3% of the time, Pallas kernels for 0%

profile of v1, /device:TPU:11, one launch (start us, length us, event | category | flops | bytes accessed | tf_op | source)
XLA Modules:
  0.0 267.4 jit_solution(4160146149028336174)
XLA Ops:
  0.9 2.1 collective-permute-start
  2.9 3.2 %collective-permute-start.1 = (f32[4,1,24,24]{3,2,1,0:T(8,128)S(1)}, f32[4,1,24,24]{3,2,1,0:T(8,128)S(1)}, u32[]{:S(2)}, u32[]{:S(2)}) collective-permute-start(f32[4,1,24,24]{3,2,1,0:T(8,128)S(1)} %get-tuple-element.9), channel_id=1, source_target_pairs={{0,8},{8,16},{16,24},{1,9},{9,17},{17,25},{2,10},{10,18},{18,26},{... | collective-permute-start | bytes 27656 | tf_op jit(solution)/shard_map/ppermute | solution.py:23
  6.2 1.6 copy.137
  8.5 1.7 copy.140
  11.2 2.2 collective-permute-start.2
  13.4 4.2 %collective-permute-start.3 = (f32[4,26,1,24]{1,3,2,0:T(8,128)S(1)}, f32[4,26,1,24]{1,3,2,0:T(8,128)S(1)}, u32[]{:S(2)}, u32[]{:S(2)}) collective-permute-start(f32[4,26,1,24]{1,3,2,0:T(8,128)S(1)} %get-tuple-element.7), channel_id=1, source_target_pairs={{0,2},{2,4},{4,6},{1,3},{3,5},{5,7},{8,10},{10,12},{12,14},{9,11},... | collective-permute-start | bytes 29960 | tf_op jit(solution)/shard_map/ppermute | solution.py:23
  19.3 4.4 %collective-permute-start.4 = (f32[4,26,26,1]{2,1,3,0:T(8,128)S(1)}, f32[4,26,26,1]{2,1,3,0:T(8,128)S(1)}, u32[]{:S(2)}, u32[]{:S(2)}) collective-permute-start(f32[4,26,26,1]{2,1,3,0:T(8,128)S(1)} %copy.145), channel_id=1, source_target_pairs={{1,0},{3,2},{5,4},{7,6},{9,8},{11,10},{13,12},{15,14},{17,16},{19,... | collective-permute-start | bytes 32456 | tf_op jit(solution)/shard_map/ppermute | solution.py:25
  25.2 2.7 copy.149
  28.3 9.4 %fusion.2 = f32[4,24,24,24]{1,3,2,0:T(8,128)S(1)} fusion(f32[4,24,24,24]{1,3,2,0:T(8,128)} %copy.149, f32[4,26,26,1]{1,3,2,0:T(1,128)S(1)} %copy.148, f32[4,26,1,24]{1,3,2,0:T(8,128)S(1)} %collective-permute-done.2, f32[4,26,1,24]{1,3,2,0:T(8,128)S(1)} %collective-permute-done.3, f32[4,1,24,24]{1,3,2,0:T(8,128)} %copy-done.1, ...), kind=kLoop, calls=%fused_computation.7 | loop fusion | flops 1437696 | bytes 778880 | tf_op jit(solution)/shard_map/sub | solution.py:101
  38.6 3.2 %collective-permute-start.6 = (f32[4,1,24,24]{3,2,1,0:T(8,128)S(1)}, f32[4,1,24,24]{3,2,1,0:T(8,128)S(1)}, u32[]{:S(2)}, u32[]{:S(2)}) collective-permute-start(f32[4,1,24,24]{3,2,1,0:T(8,128)S(1)} %copy.150), channel_id=1, source_target_pairs={{0,8},{8,16},{16,24},{1,9},{9,17},{17,25},{2,10},{10,18},{18,26},{... | collective-permute-start | bytes 27656 | tf_op jit(solution)/shard_map/ppermute | solution.py:12
  41.9 1.6 collective-permute-done.6
  44.2 4.9 %collective-permute-start.7 = (f32[4,25,1,24]{1,3,2,0:T(8,128)S(1)}, f32[4,25,1,24]{1,3,2,0:T(8,128)S(1)}, u32[]{:S(2)}, u32[]{:S(2)}) collective-permute-start(f32[4,25,1,24]{1,3,2,0:T(8,128)S(1)} %pad_maximum_fusion.35), channel_id=1, source_target_pairs={{0,2},{2,4},{4,6},{1,3},{3,5},{5,7},{8,10},{10,12},{12,14},{9,11},... | collective-permute-start | bytes 28808 | tf_op jit(solution)/shard_map/ppermute | solution.py:12
  51.8 3.8 %collective-permute-done.8 = f32[4,25,25,1]{2,1,3,0:T(8,128)S(1)} collective-permute-done((f32[4,25,25,1]{2,1,3,0:T(8,128)S(1)}, f32[4,25,25,1]{2,1,3,0:T(8,128)S(1)}, u32[]{:S(2)}, u32[]{:S(2)}) %collective-permute-start.8) | collective-permute-done | bytes 10032 | tf_op jit(solution)/shard_map/ppermute | solution.py:12
  55.8 1.8 maximum_maximum_fusion
  57.6 8.4 %slice.213 = f32[4,12,25,25]{1,3,2,0:T(8,128)} slice(f32[4,25,25,25]{1,3,2,0:T(8,128)S(1)} %maximum_maximum_fusion), slice={[0:4:1], [0:24:2], [0:25:1], [0:25:1]} | slice | bytes 240000 | tf_op jit(solution)/shard_map/slice | solution.py:48
  66.0 8.5 %slice.214 = f32[4,12,25,25]{1,3,2,0:T(8,128)} slice(f32[4,25,25,25]{1,3,2,0:T(8,128)S(1)} %maximum_maximum_fusion), slice={[0:4:1], [1:25:2], [0:25:1], [0:25:1]} | slice | bytes 240000 | tf_op jit(solution)/shard_map/slice | solution.py:49
  74.5 8.5 %slice.215 = f32[4,12,25,25]{1,3,2,0:T(8,128)} slice(f32[4,25,25,25]{1,3,2,0:T(8,128)S(1)} %maximum_maximum_fusion), slice={[0:4:1], [2:25:2], [0:25:1], [0:25:1]} | slice | bytes 240000 | tf_op jit(solution)/shard_map/slice | solution.py:50
  83.1 3.0 %multiply_add_fusion = f32[4,12,25,25]{1,3,2,0:T(8,128)S(1)} fusion(f32[4,12,25,25]{1,3,2,0:T(8,128)} %slice.215, f32[4,12,25,25]{1,3,2,0:T(8,128)} %slice.214, f32[4,12,25,25]{1,3,2,0:T(8,128)} %slice.213), kind=kLoop, calls=%fused_computation.3 | loop fusion | flops 150000 | bytes 480000 | tf_op jit(solution)/shard_map/add | solution.py:51
  87.2 3.2 %collective-permute-start.9 = (f32[4,1,12,12]{1,3,2,0:T(8,128)S(1)}, f32[4,1,12,12]{1,3,2,0:T(8,128)S(1)}, u32[]{:S(2)}, u32[]{:S(2)}) collective-permute-start(f32[4,1,12,12]{1,3,2,0:T(8,128)S(1)} %slice.265), channel_id=1, source_target_pairs={{0,8},{8,16},{16,24},{1,9},{9,17},{17,25},{2,10},{10,18},{18,26},{... | collective-permute-start | bytes 6920 | tf_op jit(solution)/shard_map/ppermute | solution.py:12
  90.4 1.9 all-gather
  92.3 7.3 %collective-permute-done.9 = f32[4,1,12,12]{1,3,2,0:T(8,128)S(1)} collective-permute-done((f32[4,1,12,12]{1,3,2,0:T(8,128)S(1)}, f32[4,1,12,12]{1,3,2,0:T(8,128)S(1)}, u32[]{:S(2)}, u32[]{:S(2)}) %collective-permute-start.9) | collective-permute-done | bytes 2336 | tf_op jit(solution)/shard_map/ppermute | solution.py:12
  99.7 4.9 %collective-permute-start.10 = (f32[4,13,1,12]{1,3,2,0:T(8,128)S(1)}, f32[4,13,1,12]{1,3,2,0:T(8,128)S(1)}, u32[]{:S(2)}, u32[]{:S(2)}) collective-permute-start(f32[4,13,1,12]{1,3,2,0:T(8,128)S(1)} %pad_maximum_fusion.39), channel_id=1, source_target_pairs={{0,2},{2,4},{4,6},{1,3},{3,5},{5,7},{8,10},{10,12},{12,14},{9,11},... | collective-permute-start | bytes 7496 | tf_op jit(solution)/shard_map/ppermute | solution.py:12
  115.0 2.6 collective-permute-start.12
  118.5 1.8 all-gather.1
  120.8 1.9 collective-permute-start.13
  122.9 3.7 %collective-permute-done.13 = f32[4,30]{1,0:T(4,128)S(1)} collective-permute-done((f32[4,30]{1,0:T(4,128)S(1)}, f32[4,30]{1,0:T(4,128)S(1)}, u32[]{:S(2)}, u32[]{:S(2)}) %collective-permute-start.13) | collective-permute-done | bytes 512 | tf_op jit(solution)/shard_map/ppermute | solution.py:12
  126.8 11.4 %all-reduce = f32[4,240]{1,0:T(4,128)S(1)} all-reduce(f32[4,240]{1,0:T(4,128)S(1)} %fusion.36), channel_id=3, replica_groups=mesh['gx'=4,'gy'=4,'gz'=2] {'gy','gz'}, use_global_device_ids=true, to_apply=%region_0.1.clone | all-reduce | flops 960 | bytes 7680
  138.5 2.1 collective-permute-start.14
  140.6 2.2 collective-permute-done.14
  143.1 40.6 %all-reduce.1 = f32[4,1152]{1,0:T(4,128)S(1)} all-reduce(f32[4,1152]{1,0:T(4,128)S(1)} %fusion.68), channel_id=4, replica_groups=mesh['gx'=4,'gy'=4,'gz'=2] {'gx','gy','gz'}, use_global_device_ids=true, to_apply=%region_1.2.clone | all-reduce | flops 4608 | bytes 36864
  184.0 12.3 %all_to_all.5 = f32[32,1,144]{2,1,0:T(1,128)S(1)} all-to-all(f32[32,1,144]{2,1,0:T(1,128)S(1)} %reshape.115), channel_id=1, replica_groups=mesh['gx'=4,'gy'=4,'gz'=2] {'gx','gy','gz'}, dimensions={0} | all-to-all | bytes 36864 | tf_op jit(solution)/shard_map/all_to_all | solution.py:172
  198.0 2.3 collective-permute-start.15
  200.2 2.1 collective-permute-done.15
  202.5 10.3 %all-gather.2 = f32[8,30,4]{1,2,0:T(4,128)S(1)} all-gather(f32[1,30,4]{1,2,0:T(4,128)S(1)} %fusion.9), channel_id=1, replica_groups=mesh['gx'=4,'gy'=4,'gz'=2] {'gy','gz'}, dimensions={0}, use_global_device_ids=true | all-gather | bytes 4320 | tf_op jit(solution)/shard_map/all_gather | solution.py:178
  213.1 3.1 %collective-permute-start.16 = (f32[4,30]{1,0:T(4,128)S(1)}, f32[4,30]{1,0:T(4,128)S(1)}, u32[]{:S(2)}, u32[]{:S(2)}) collective-permute-start(f32[4,30]{1,0:T(4,128)S(1)} %fusion.34), channel_id=1, source_target_pairs={{0,2},{2,4},{4,6},{1,3},{3,5},{5,7},{8,10},{10,12},{12,14},{9,11},... | collective-permute-start | bytes 1448 | tf_op jit(solution)/shard_map/ppermute | solution.py:12
  217.8 2.8 %all-gather.3 = f32[2,25,4]{1,2,0:T(4,128)S(1)} all-gather(f32[1,25,4]{1,2,0:T(4,128)S(1)} %fusion.8), channel_id=1, replica_groups=mesh['gx'=4,'gy'=4,'gz'=2] {'gz'}, dimensions={0}, use_global_device_ids=true | all-gather | bytes 1200 | tf_op jit(solution)/shard_map/all_gather | solution.py:187
  222.4 1.6 collective-permute-done.17
  226.1 1.9 collective-permute-start.18
  228.0 2.5 collective-permute-done.18
  230.6 1.9 collective-permute-start.19
  232.5 3.4 %collective-permute-done.19 = f32[4,7,1,6]{3,2,1,0:T(1,128)S(1)} collective-permute-done((f32[4,7,1,6]{3,2,1,0:T(1,128)S(1)}, f32[4,7,1,6]{3,2,1,0:T(1,128)S(1)}, u32[]{:S(2)}, u32[]{:S(2)}) %collective-permute-start.19) | collective-permute-done | bytes 704 | tf_op jit(solution)/shard_map/ppermute | solution.py:12
  236.0 4.4 %collective-permute-start.20 = (f32[4,7,7,1]{3,2,1,0:T(8,128)S(1)}, f32[4,7,7,1]{3,2,1,0:T(8,128)S(1)}, u32[]{:S(2)}, u32[]{:S(2)}) collective-permute-start(f32[4,7,7,1]{3,2,1,0:T(8,128)S(1)} %pad_maximum_fusion.26), channel_id=1, source_target_pairs={{1,0},{3,2},{5,4},{7,6},{9,8},{11,10},{13,12},{15,14},{17,16},{19,... | collective-permute-start | bytes 2360 | tf_op jit(solution)/shard_map/ppermute | solution.py:12
  242.7 1.9 collective-permute-start.21
  244.6 2.6 collective-permute-done.21
  247.3 1.9 collective-permute-start.22
  249.3 8.4 %collective-permute-done.22 = f32[4,13,1,12]{2,0,3,1:T(4,128)S(1)} collective-permute-done((f32[4,13,1,12]{2,0,3,1:T(4,128)S(1)}, f32[4,13,1,12]{2,0,3,1:T(4,128)S(1)}, u32[]{:S(2)}, u32[]{:S(2)}) %collective-permute-start.22) | collective-permute-done | bytes 2528 | tf_op jit(solution)/shard_map/ppermute | solution.py:12
  257.8 4.3 %collective-permute-start.23 = (f32[4,13,13,1]{2,0,3,1:T(4,128)S(1)}, f32[4,13,13,1]{2,0,3,1:T(4,128)S(1)}, u32[]{:S(2)}, u32[]{:S(2)}) collective-permute-start(f32[4,13,13,1]{2,0,3,1:T(4,128)S(1)} %pad_maximum_fusion.40), channel_id=1, source_target_pairs={{1,0},{3,2},{5,4},{7,6},{9,8},{11,10},{13,12},{15,14},{17,16},{19,... | collective-permute-start | bytes 8120 | tf_op jit(solution)/shard_map/ppermute | solution.py:12
  266.0 1.4 copy.179
  (167 shorter events, 37.7 us)
Async XLA Ops:
  0.0 142.9 %copy-start = (f32[36,1152]{1,0:T(8,128)S(1)}, f32[36,1152]{1,0:T(8,128)}, u32[]{:S(2)}) copy-start(f32[36,1152]{1,0:T(8,128)} %param.27) | copy-start | bytes 497668
  0.9 6.9 %collective-permute-start = (f32[4,1,24,24]{3,2,1,0:T(8,128)S(1)}, f32[4,1,24,24]{3,2,1,0:T(8,128)S(1)}, u32[]{:S(2)}, u32[]{:S(2)}) collective-permute-start(f32[4,1,24,24]{3,2,1,0:T(8,128)S(1)} %get-tuple-element.10), channel_id=1, source_target_pairs={{8,0},{16,8},{24,16},{9,1},{17,9},{25,17},{10,2},{18,10},{26,18},{... | collective-permute-start | bytes 27656 | tf_op jit(solution)/shard_map/ppermute | solution.py:25
  2.9 5.5 %collective-permute-start.1 = (f32[4,1,24,24]{3,2,1,0:T(8,128)S(1)}, f32[4,1,24,24]{3,2,1,0:T(8,128)S(1)}, u32[]{:S(2)}, u32[]{:S(2)}) collective-permute-start(f32[4,1,24,24]{3,2,1,0:T(8,128)S(1)} %get-tuple-element.9), channel_id=1, source_target_pairs={{0,8},{8,16},{16,24},{1,9},{9,17},{17,25},{2,10},{10,18},{18,26},{... | collective-permute-start | bytes 27656 | tf_op jit(solution)/shard_map/ppermute | solution.py:23
  8.5 10.7 %copy-start.1 = (f32[4,1,24,24]{1,3,2,0:T(8,128)}, f32[4,1,24,24]{1,3,2,0:T(8,128)S(1)}, u32[]{:S(2)}) copy-start(f32[4,1,24,24]{1,3,2,0:T(8,128)S(1)} %copy.139) | copy-start | bytes 27652
  10.2 8.5 %copy-start.2 = (f32[4,1,24,24]{1,3,2,0:T(8,128)S(1)}, f32[4,1,24,24]{1,3,2,0:T(8,128)}, u32[]{:S(2)}) copy-start(f32[4,1,24,24]{1,3,2,0:T(8,128)} %copy.140) | copy-start | bytes 27652
  11.2 6.3 %collective-permute-start.2 = (f32[4,26,1,24]{1,3,2,0:T(8,128)S(1)}, f32[4,26,1,24]{1,3,2,0:T(8,128)S(1)}, u32[]{:S(2)}, u32[]{:S(2)}) collective-permute-start(f32[4,26,1,24]{1,3,2,0:T(8,128)S(1)} %get-tuple-element.8), channel_id=1, source_target_pairs={{2,0},{4,2},{6,4},{3,1},{5,3},{7,5},{10,8},{12,10},{14,12},{11,9},... | collective-permute-start | bytes 29960 | tf_op jit(solution)/shard_map/ppermute | solution.py:25
  13.4 11.8 %copy-start.4 = (f32[24,24,24]{2,1,0:T(8,128)S(1)}, f32[24,24,24]{2,1,0:T(8,128)}, u32[]{:S(2)}) copy-start(f32[24,24,24]{2,1,0:T(8,128)} %param.16) | copy-start | bytes 165892
  13.4 5.3 %collective-permute-start.3 = (f32[4,26,1,24]{1,3,2,0:T(8,128)S(1)}, f32[4,26,1,24]{1,3,2,0:T(8,128)S(1)}, u32[]{:S(2)}, u32[]{:S(2)}) collective-permute-start(f32[4,26,1,24]{1,3,2,0:T(8,128)S(1)} %get-tuple-element.7), channel_id=1, source_target_pairs={{0,2},{2,4},{4,6},{1,3},{3,5},{5,7},{8,10},{10,12},{12,14},{9,11},... | collective-permute-start | bytes 29960 | tf_op jit(solution)/shard_map/ppermute | solution.py:23
  19.3 8.7 %collective-permute-start.4 = (f32[4,26,26,1]{2,1,3,0:T(8,128)S(1)}, f32[4,26,26,1]{2,1,3,0:T(8,128)S(1)}, u32[]{:S(2)}, u32[]{:S(2)}) collective-permute-start(f32[4,26,26,1]{2,1,3,0:T(8,128)S(1)} %copy.145), channel_id=1, source_target_pairs={{1,0},{3,2},{5,4},{7,6},{9,8},{11,10},{13,12},{15,14},{17,16},{19,... | collective-permute-start | bytes 32456 | tf_op jit(solution)/shard_map/ppermute | solution.py:25
  23.9 4.3 %collective-permute-start.5 = (f32[4,26,26,1]{2,1,3,0:T(8,128)S(1)}, f32[4,26,26,1]{2,1,3,0:T(8,128)S(1)}, u32[]{:S(2)}, u32[]{:S(2)}) collective-permute-start(f32[4,26,26,1]{2,1,3,0:T(8,128)S(1)} %copy.147), channel_id=1, source_target_pairs={{0,1},{2,3},{4,5},{6,7},{8,9},{10,11},{12,13},{14,15},{16,17},{18,... | collective-permute-start | bytes 32456 | tf_op jit(solution)/shard_map/ppermute | solution.py:23
  38.6 4.8 %collective-permute-start.6 = (f32[4,1,24,24]{3,2,1,0:T(8,128)S(1)}, f32[4,1,24,24]{3,2,1,0:T(8,128)S(1)}, u32[]{:S(2)}, u32[]{:S(2)}) collective-permute-start(f32[4,1,24,24]{3,2,1,0:T(8,128)S(1)} %copy.150), channel_id=1, source_target_pairs={{0,8},{8,16},{16,24},{1,9},{9,17},{17,25},{2,10},{10,18},{18,26},{... | collective-permute-start | bytes 27656 | tf_op jit(solution)/shard_map/ppermute | solution.py:12
  44.1 11.6 %copy-start.3 = (f32[4,1,24,24]{1,3,2,0:T(8,128)}, f32[4,1,24,24]{1,3,2,0:T(8,128)S(1)}, u32[]{:S(2)}) copy-start(f32[4,1,24,24]{1,3,2,0:T(8,128)S(1)} %copy.151) | copy-start | bytes 27652
  44.1 5.0 %copy-start.14 = (s32[1,1,1,216]{3,2,1,0:T(1,128)S(1)}, s32[1,1,1,216]{3,2,1,0:T(1,128)}, u32[]{:S(2)}) copy-start(s32[1,1,1,216]{3,2,1,0:T(1,128)} %param.17) | copy-start | bytes 2596
  44.2 6.0 %collective-permute-start.7 = (f32[4,25,1,24]{1,3,2,0:T(8,128)S(1)}, f32[4,25,1,24]{1,3,2,0:T(8,128)S(1)}, u32[]{:S(2)}, u32[]{:S(2)}) collective-permute-start(f32[4,25,1,24]{1,3,2,0:T(8,128)S(1)} %pad_maximum_fusion.35), channel_id=1, source_target_pairs={{0,2},{2,4},{4,6},{1,3},{3,5},{5,7},{8,10},{10,12},{12,14},{9,11},... | collective-permute-start | bytes 28808 | tf_op jit(solution)/shard_map/ppermute | solution.py:12
  50.5 5.1 %collective-permute-start.8 = (f32[4,25,25,1]{2,1,3,0:T(8,128)S(1)}, f32[4,25,25,1]{2,1,3,0:T(8,128)S(1)}, u32[]{:S(2)}, u32[]{:S(2)}) collective-permute-start(f32[4,25,25,1]{2,1,3,0:T(8,128)S(1)} %copy.152), channel_id=1, source_target_pairs={{0,1},{2,3},{4,5},{6,7},{8,9},{10,11},{12,13},{14,15},{16,17},{18,... | collective-permute-start | bytes 30008 | tf_op jit(solution)/shard_map/ppermute | solution.py:12
  86.9 3.5 %copy-start.13 = (f32[1,1,25,50]{3,1,2,0:T(1,128)S(1)}, f32[1,1,25,50]{3,1,2,0:T(1,128)}, u32[]{:S(2)}) copy-start(f32[1,1,25,50]{3,1,2,0:T(1,128)} %param.22) | copy-start | bytes 15004
  87.0 20.1 %copy-start.15 = (u32[32]{0:T(128)S(1)}, u32[32]{0:T(128)}, u32[]{:S(2)}) copy-start(u32[32]{0:T(128)} %constant.32) | copy-start | bytes 388
  87.2 12.4 %collective-permute-start.9 = (f32[4,1,12,12]{1,3,2,0:T(8,128)S(1)}, f32[4,1,12,12]{1,3,2,0:T(8,128)S(1)}, u32[]{:S(2)}, u32[]{:S(2)}) collective-permute-start(f32[4,1,12,12]{1,3,2,0:T(8,128)S(1)} %slice.265), channel_id=1, source_target_pairs={{0,8},{8,16},{16,24},{1,9},{9,17},{17,25},{2,10},{10,18},{18,26},{... | collective-permute-start | bytes 6920 | tf_op jit(solution)/shard_map/ppermute | solution.py:12
  99.7 5.9 %collective-permute-start.10 = (f32[4,13,1,12]{1,3,2,0:T(8,128)S(1)}, f32[4,13,1,12]{1,3,2,0:T(8,128)S(1)}, u32[]{:S(2)}, u32[]{:S(2)}) collective-permute-start(f32[4,13,1,12]{1,3,2,0:T(8,128)S(1)} %pad_maximum_fusion.39), channel_id=1, source_target_pairs={{0,2},{2,4},{4,6},{1,3},{3,5},{5,7},{8,10},{10,12},{12,14},{9,11},... | collective-permute-start | bytes 7496 | tf_op jit(solution)/shard_map/ppermute | solution.py:12
  105.7 3.8 %collective-permute-start.11 = (f32[4,13,13,1]{1,3,2,0:T(1,128)S(1)}, f32[4,13,13,1]{1,3,2,0:T(1,128)S(1)}, u32[]{:S(2)}, u32[]{:S(2)}) collective-permute-start(f32[4,13,13,1]{1,3,2,0:T(1,128)S(1)} %pad_maximum_fusion.42), channel_id=1, source_target_pairs={{0,1},{2,3},{4,5},{6,7},{8,9},{10,11},{12,13},{14,15},{16,17},{18,... | collective-permute-start | bytes 8120 | tf_op jit(solution)/shard_map/ppermute | solution.py:12
  112.6 2.0 copy-start.5
  112.7 2.1 copy-start.9
  112.7 5.0 %copy-start.6 = (f32[1,1,1,125,72]{3,4,2,1,0:T(8,128)S(1)}, f32[1,1,1,125,72]{3,4,2,1,0:T(8,128)}, u32[]{:S(2)}) copy-start(f32[1,1,1,125,72]{3,4,2,1,0:T(8,128)} %param.21) | copy-start | bytes 108004
  112.7 5.1 %copy-start.8 = (f32[1,1,1,125,60]{3,2,4,1,0:T(1,128)S(1)}, f32[1,1,1,125,60]{3,2,4,1,0:T(1,128)}, u32[]{:S(2)}) copy-start(f32[1,1,1,125,60]{3,2,4,1,0:T(1,128)} %param.20) | copy-start | bytes 90004
  112.7 7.9 %copy-start.10 = (f32[1,1,1,25,60]{4,2,3,1,0:T(1,128)S(1)}, f32[1,1,1,25,60]{4,2,3,1,0:T(1,128)}, u32[]{:S(2)}) copy-start(f32[1,1,1,25,60]{4,2,3,1,0:T(1,128)} %param.23) | copy-start | bytes 18004
  112.7 10.0 %copy-start.11 = (f32[1,1,1,25,72]{4,2,3,1,0:T(1,128)S(1)}, f32[1,1,1,25,72]{4,2,3,1,0:T(1,128)}, u32[]{:S(2)}) copy-start(f32[1,1,1,25,72]{4,2,3,1,0:T(1,128)} %param.24) | copy-start | bytes 21604
  112.7 13.9 %copy-start.7 = (f32[1,30,240]{2,0,1:T(1,128)S(1)}, f32[1,30,240]{2,0,1:T(1,128)}, u32[]{:S(2)}) copy-start(f32[1,30,240]{2,0,1:T(1,128)} %param.25) | copy-start | bytes 86404
  112.7 25.5 %copy-start.12 = (f32[1,1,1,30,72]{4,2,3,1,0:T(1,128)S(1)}, f32[1,1,1,30,72]{4,2,3,1,0:T(1,128)}, u32[]{:S(2)}) copy-start(f32[1,1,1,30,72]{4,2,3,1,0:T(1,128)} %param.26) | copy-start | bytes 25924
  115.0 3.4 %collective-permute-start.12 = (f32[4,25]{1,0:T(4,128)S(1)}, f32[4,25]{1,0:T(4,128)S(1)}, u32[]{:S(2)}, u32[]{:S(2)}) collective-permute-start(f32[4,25]{1,0:T(4,128)S(1)} %slice.237), channel_id=1, source_target_pairs={{1,0},{3,2},{5,4},{7,6},{9,8},{11,10},{13,12},{15,14},{17,16},{19,... | collective-permute-start | bytes 1208 | tf_op jit(solution)/shard_map/ppermute | solution.py:12
  120.8 5.8 %collective-permute-start.13 = (f32[4,30]{1,0:T(4,128)S(1)}, f32[4,30]{1,0:T(4,128)S(1)}, u32[]{:S(2)}, u32[]{:S(2)}) collective-permute-start(f32[4,30]{1,0:T(4,128)S(1)} %slice.240), channel_id=1, source_target_pairs={{2,0},{4,2},{6,4},{3,1},{5,3},{7,5},{10,8},{12,10},{14,12},{11,9},... | collective-permute-start | bytes 1448 | tf_op jit(solution)/shard_map/ppermute | solution.py:12
  138.5 4.3 %collective-permute-start.14 = (f32[4,36]{1,0:T(4,128)S(1)}, f32[4,36]{1,0:T(4,128)S(1)}, u32[]{:S(2)}, u32[]{:S(2)}) collective-permute-start(f32[4,36]{1,0:T(4,128)S(1)} %slice.243), channel_id=1, source_target_pairs={{8,0},{16,8},{24,16},{9,1},{17,9},{25,17},{10,2},{18,10},{26,18},{... | collective-permute-start | bytes 1736 | tf_op jit(solution)/shard_map/ppermute | solution.py:12
  198.0 4.4 %collective-permute-start.15 = (f32[4,36]{1,0:T(4,128)S(1)}, f32[4,36]{1,0:T(4,128)S(1)}, u32[]{:S(2)}, u32[]{:S(2)}) collective-permute-start(f32[4,36]{1,0:T(4,128)S(1)} %fusion.86), channel_id=1, source_target_pairs={{0,8},{8,16},{16,24},{1,9},{9,17},{17,25},{2,10},{10,18},{18,26},{... | collective-permute-start | bytes 1736 | tf_op jit(solution)/shard_map/ppermute | solution.py:12
  213.1 4.3 %collective-permute-start.16 = (f32[4,30]{1,0:T(4,128)S(1)}, f32[4,30]{1,0:T(4,128)S(1)}, u32[]{:S(2)}, u32[]{:S(2)}) collective-permute-start(f32[4,30]{1,0:T(4,128)S(1)} %fusion.34), channel_id=1, source_target_pairs={{0,2},{2,4},{4,6},{1,3},{3,5},{5,7},{8,10},{10,12},{12,14},{9,11},... | collective-permute-start | bytes 1448 | tf_op jit(solution)/shard_map/ppermute | solution.py:12
  220.8 3.1 %collective-permute-start.17 = (f32[4,25]{1,0:T(4,128)S(1)}, f32[4,25]{1,0:T(4,128)S(1)}, u32[]{:S(2)}, u32[]{:S(2)}) collective-permute-start(f32[4,25]{1,0:T(4,128)S(1)} %fusion.50), channel_id=1, source_target_pairs={{0,1},{2,3},{4,5},{6,7},{8,9},{10,11},{12,13},{14,15},{16,17},{18,... | collective-permute-start | bytes 1208 | tf_op jit(solution)/shard_map/ppermute | solution.py:12
  226.1 4.5 %collective-permute-start.18 = (f32[4,1,6,6]{3,2,1,0:T(8,128)S(1)}, f32[4,1,6,6]{3,2,1,0:T(8,128)S(1)}, u32[]{:S(2)}, u32[]{:S(2)}) collective-permute-start(f32[4,1,6,6]{3,2,1,0:T(8,128)S(1)} %slice.270), channel_id=1, source_target_pairs={{8,0},{16,8},{24,16},{9,1},{17,9},{25,17},{10,2},{18,10},{26,18},{... | collective-permute-start | bytes 1736 | tf_op jit(solution)/shard_map/ppermute | solution.py:12
  230.6 5.4 %collective-permute-start.19 = (f32[4,7,1,6]{3,2,1,0:T(1,128)S(1)}, f32[4,7,1,6]{3,2,1,0:T(1,128)S(1)}, u32[]{:S(2)}, u32[]{:S(2)}) collective-permute-start(f32[4,7,1,6]{3,2,1,0:T(1,128)S(1)} %slice.271), channel_id=1, source_target_pairs={{2,0},{4,2},{6,4},{3,1},{5,3},{7,5},{10,8},{12,10},{14,12},{11,9},... | collective-permute-start | bytes 2024 | tf_op jit(solution)/shard_map/ppermute | solution.py:12
  236.0 5.3 %collective-permute-start.20 = (f32[4,7,7,1]{3,2,1,0:T(8,128)S(1)}, f32[4,7,7,1]{3,2,1,0:T(8,128)S(1)}, u32[]{:S(2)}, u32[]{:S(2)}) collective-permute-start(f32[4,7,7,1]{3,2,1,0:T(8,128)S(1)} %pad_maximum_fusion.26), channel_id=1, source_target_pairs={{1,0},{3,2},{5,4},{7,6},{9,8},{11,10},{13,12},{15,14},{17,16},{19,... | collective-permute-start | bytes 2360 | tf_op jit(solution)/shard_map/ppermute | solution.py:12
  242.7 4.6 %collective-permute-start.21 = (f32[4,1,12,12]{2,0,3,1:T(4,128)S(1)}, f32[4,1,12,12]{2,0,3,1:T(4,128)S(1)}, u32[]{:S(2)}, u32[]{:S(2)}) collective-permute-start(f32[4,1,12,12]{2,0,3,1:T(4,128)S(1)} %slice.278), channel_id=1, source_target_pairs={{8,0},{16,8},{24,16},{9,1},{17,9},{25,17},{10,2},{18,10},{26,18},{... | collective-permute-start | bytes 6920 | tf_op jit(solution)/shard_map/ppermute | solution.py:12
  247.3 10.4 %collective-permute-start.22 = (f32[4,13,1,12]{2,0,3,1:T(4,128)S(1)}, f32[4,13,1,12]{2,0,3,1:T(4,128)S(1)}, u32[]{:S(2)}, u32[]{:S(2)}) collective-permute-start(f32[4,13,1,12]{2,0,3,1:T(4,128)S(1)} %pad_maximum_fusion.22), channel_id=1, source_target_pairs={{2,0},{4,2},{6,4},{3,1},{5,3},{7,5},{10,8},{12,10},{14,12},{11,9},... | collective-permute-start | bytes 7496 | tf_op jit(solution)/shard_map/ppermute | solution.py:12
  257.8 5.1 %collective-permute-start.23 = (f32[4,13,13,1]{2,0,3,1:T(4,128)S(1)}, f32[4,13,13,1]{2,0,3,1:T(4,128)S(1)}, u32[]{:S(2)}, u32[]{:S(2)}) collective-permute-start(f32[4,13,13,1]{2,0,3,1:T(4,128)S(1)} %pad_maximum_fusion.40), channel_id=1, source_target_pairs={{1,0},{3,2},{5,4},{7,6},{9,8},{11,10},{13,12},{15,14},{17,16},{19,... | collective-permute-start | bytes 8120 | tf_op jit(solution)/shard_map/ppermute | solution.py:12
